TPU v7x, 64 devices: a 2x2x8 block of a 4x4x8 slice. The times are simulated.
64 devices in a mesh: dp: 4 (over x, y), sp: 16 (over z, core).
Axes of the slice: x: 2, y: 2, z: 8, core: 2. Of those that a mesh axis runs over, the one named last changes fastest.
The devices are a block of a 4x4x8 slice.
Arguments:
- tokens: bfloat16 [384, 4096], P('dp'), parts along dimension 0
- w_query: bfloat16 [4096, 4096], replicated
- w_key: bfloat16 [4096, 256], replicated
- w_value: bfloat16 [4096, 256], replicated
- w_out: bfloat16 [4096, 4096], P('sp')
- k_cache: bfloat16 [384, 1024, 256], P('dp', 'sp'), parts along dimension 0
- v_cache: bfloat16 [384, 1024, 256], P('dp', 'sp'), parts along dimension 0
- positions: int32 [384], P('dp'), parts along dimension 0
Outputs:
- output 1: bfloat16 [384, 4096], P('dp'), parts along dimension 0
- output 2: bfloat16 [384, 1024, 256], P('dp', 'sp'), parts along dimension 0
- output 3: bfloat16 [384, 1024, 256], P('dp', 'sp'), parts along dimension 0
There are 4 independent parts. A program takes and returns all parts, laid end to end along the dimension named above; an argument that names none is the same for every part.
All inputs are finite; a program needn't handle non-finite values.
Results may differ from a plain program's by a relative error of at most 0.00458535.
Values are sent between devices in bfloat16 or wider.
A program may use at most 768 MiB of HBM per device.

v0:
```python
import jax
import jax.numpy as jnp
from jax import lax
from jax.sharding import PartitionSpec as P


def solution(mesh):
    def local_step(tokens, w_query, w_key, w_value, w_out, k_cache, v_cache, positions):
        n_rows, seq_local, head_dim = k_cache.shape
        q_width = w_query.shape[1]
        n_heads = q_width // head_dim
        rows_local = w_out.shape[0]
        shard_idx = lax.axis_index('sp')
        queries = jnp.dot(tokens, w_query, preferred_element_type=jnp.float32).astype(jnp.bfloat16).reshape(n_rows, n_heads, head_dim)
        key_new = jnp.dot(tokens, w_key, preferred_element_type=jnp.float32).astype(jnp.bfloat16)
        value_new = jnp.dot(tokens, w_value, preferred_element_type=jnp.float32).astype(jnp.bfloat16)
        local_pos = positions - shard_idx * seq_local
        slot_ids = jnp.arange(seq_local)
        hit_mask = (slot_ids[None, :] == local_pos[:, None])[:, :, None]
        k_upd = jnp.where(hit_mask, key_new[:, None, :], k_cache)
        v_upd = jnp.where(hit_mask, value_new[:, None, :], v_cache)
        scores = jnp.einsum('bhd,btd->bht', queries, k_upd, preferred_element_type=jnp.float32) * head_dim ** -0.5
        valid_mask = (slot_ids[None, :] <= local_pos[:, None])[:, None, :]
        scores = jnp.where(valid_mask, scores, -jnp.inf)
        row_peak = jnp.maximum(jnp.max(scores, axis=2), -1e30)
        weights = jnp.exp(scores - row_peak[:, :, None])
        weight_sum = jnp.sum(weights, axis=2)
        value_sum = jnp.einsum('bht,btd->bhd', weights.astype(jnp.bfloat16), v_upd, preferred_element_type=jnp.float32)
        peak_all = lax.pmax(row_peak, 'sp')
        rescale = jnp.exp(row_peak - peak_all)
        weight_all = lax.psum(weight_sum * rescale, 'sp')
        value_all = lax.psum(value_sum * rescale[:, :, None], 'sp')
        attn_heads = (value_all / weight_all[:, :, None]).astype(jnp.bfloat16).reshape(n_rows, q_width)
        attn_local = lax.dynamic_slice_in_dim(attn_heads, shard_idx * rows_local, rows_local, axis=1)
        partial = jnp.dot(attn_local, w_out, preferred_element_type=jnp.float32)
        attn_out = lax.psum(partial, 'sp').astype(jnp.bfloat16)
        return attn_out, k_upd, v_upd

    cache_spec = P('dp', 'sp', None)
    return jax.shard_map(local_step, mesh=mesh, in_specs=(P('dp', None), P(), P(), P(), P('sp', None), cache_spec, cache_spec, P('dp')), out_specs=(P('dp', None), cache_spec, cache_spec), check_vma=False)
```

profile of v0, /device:TPU:22, one launch (start us, length us, event | category | flops | bytes accessed | tf_op | source)
XLA Modules:
  0.0 262.2 jit_solution(3876014765104320793)
XLA Ops:
  7.2 0.0 copy-start
  7.2 0.0 copy-start.2
  7.2 0.1 all-reduce.3.cloned.1.call-start
  7.3 0.0 copy-start.5
  7.3 0.8 broadcast_subtract_fusion
  8.1 0.1 iota_compare_fusion.1
  8.2 2.3 convolution_convert_fusion.2
  10.5 0.0 copy-done.2
  10.5 0.0 copy-done.5
  10.6 0.5 convolution_convert_fusion.1
  11.0 0.0 copy-start.3
  11.0 0.0 copy-start.4
  11.0 13.6 %convolution_convert_fusion = bf16[96,4096]{1,0:T(8,128)(2,1)S(1)} fusion(bf16[96,4096]{1,0:T(8,128)(2,1)S(1)} %copy-done.2, bf16[4096,4096]{1,0:T(8,128)(2,1)} %param.9), kind=kOutput, calls=%fused_computation | convolution fusion | flops 3221618688 | bytes 35127296 | tf_op jit(solution)/shard_map/dot_general | solution.py:14
  24.6 0.2 copy.11
  24.8 0.0 copy-done.3
  24.8 0.0 copy-done.4
  24.8 2.6 broadcast_select_fusion.1
  27.4 0.0 copy-start.1
  27.4 1.0 fusion.9
  28.4 0.7 copy-done.1
  29.1 52.5 %pmax.7 = f32[96,16]{1,0:T(8,128)S(1)} all-reduce(f32[96,16]{1,0:T(8,128)S(1)} %broadcast_maximum_fusion), channel_id=1, replica_groups=mesh['dp'=4,'sp'=16] {'sp'}, use_global_device_ids=true, to_apply=%region_1.2 | all-reduce | flops 1536 | bytes 12288 | tf_op jit(solution)/shard_map/pmax | solution.py:29
  81.6 0.5 fusion.1
  82.1 3.7 %convolution_multiply_fusion = f32[96,16,256]{2,1,0:T(8,128)} fusion(bf16[96,64,256]{2,1,0:T(8,128)(2,1)} %get-tuple-element.6, f32[96,16]{1,0:T(8,128)S(1)} %get-tuple-element.4, f32[96,16,64]{2,1,0:T(8,128)S(1)} %get-tuple-element.10, f32[96,16]{1,0:T(8,128)S(1)} %broadcast_maximum_fusion), kind=kOutput, calls=%fused_computation.4 | convolution fusion | flops 50921472 | bytes 5124096 | tf_op jit(solution)/shard_map/bht,btd->bhd/dot_general | solution.py:28
  85.8 0.1 all-reduce.3.cloned.1.call-update
  85.9 46.0 %psum.22 = f32[96,16]{1,0:T(8,128)S(1)} all-reduce(f32[96,16]{1,0:T(8,128)S(1)} %get-tuple-element.3), channel_id=1, replica_groups=mesh['dp'=4,'sp'=16] {'sp'}, use_global_device_ids=true, to_apply=%region_4.5 | all-reduce | flops 1536 | bytes 12288 | tf_op jit(solution)/shard_map/psum | solution.py:31
  131.8 58.5 %all-reduce.3.cloned.1.call-done = f32[96,16,256]{2,1,0:T(8,128)} async-done(((f32[96,16,256]{2,1,0:T(8,128)}), f32[96,16,256]{2,1,0:T(8,128)}) %all-reduce.3.cloned.1.call-update) | async-done | bytes 1572880 | tf_op jit(solution)/shard_map/psum | solution.py:32
  190.3 1.7 divide_convert_fusion
  192.0 0.3 copy.12
  192.3 0.0 copy-done
  192.3 1.6 fusion.5
  193.9 61.5 %all-reduce.4 = bf16[96,4096]{1,0:T(8,128)(2,1)} all-reduce(f32[96,4096]{1,0:T(8,128)} %fusion.5), channel_id=1, replica_groups=mesh['dp'=4,'sp'=16] {'sp'}, use_global_device_ids=true, to_apply=%region_5.6 | all-reduce | flops 393216 | bytes 2359296 | tf_op jit(solution)/shard_map/psum | solution.py:36
  (2 shorter events, 0.0 us)
Async XLA Ops:
  7.2 185.1 %copy-start = (bf16[256,4096]{1,0:T(8,128)(2,1)S(1)}, bf16[256,4096]{1,0:T(8,128)(2,1)}, u32[]{:S(2)}) copy-start(bf16[256,4096]{1,0:T(8,128)(2,1)} %param.12) | copy-start | bytes 6291460
  7.2 3.3 %copy-start.2 = (bf16[96,4096]{1,0:T(8,128)(2,1)S(1)}, bf16[96,4096]{1,0:T(8,128)(2,1)}, u32[]{:S(2)}) copy-start(bf16[96,4096]{1,0:T(8,128)(2,1)} %param.8) | copy-start | bytes 2359300
  7.2 183.1 %all-reduce.3.cloned.1.call-start = ((), (), s32[]{:S(2)}) async-start(), calls=%async_computation | async-start | bytes 3145728 | tf_op jit(solution)/shard_map/psum | solution.py:32
  7.3 3.3 %copy-start.5 = (bf16[4096,256]{1,0:T(8,128)(2,1)S(1)}, bf16[4096,256]{1,0:T(8,128)(2,1)}, u32[]{:S(2)}) copy-start(bf16[4096,256]{1,0:T(8,128)(2,1)} %param.11) | copy-start | bytes 6291460
  11.0 13.8 %copy-start.3 = (bf16[96,64,256]{2,1,0:T(8,128)(2,1)S(1)}, bf16[96,64,256]{2,1,0:T(8,128)(2,1)}, u32[]{:S(2)}) copy-start(bf16[96,64,256]{2,1,0:T(8,128)(2,1)} %param.13) | copy-start | bytes 9437188
  11.0 13.8 %copy-start.4 = (bf16[96,64,256]{2,1,0:T(8,128)(2,1)S(1)}, bf16[96,64,256]{2,1,0:T(8,128)(2,1)}, u32[]{:S(2)}) copy-start(bf16[96,64,256]{2,1,0:T(8,128)(2,1)} %param.14) | copy-start | bytes 9437188
  27.4 1.7 copy-start.1
Sparse Core Ops, SparseCore 0:
  86.0 104.2 all-reduce.2
where the time goes:
time: 262 us
  blocking collectives  160 us (61%)
  waiting for transfers between devices  58.5 us (22%)
  matrix products  22.7 us (9%)
  between operations  14.2 us (5%)
  other arithmetic  5.72 us (2%)
    psum x1, blocking collectives, local_step(): attn_out = lax.psum(partial, 'sp').astype(jnp.bfloat16)  61.5 us
    psum x1, waiting for transfers between devices, local_step(): value_all = lax.psum(value_sum * rescale[:, :, None], 'sp')  58.5 us
    pmax x1, blocking collectives, local_step(): peak_all = lax.pmax(row_peak, 'sp')  52.5 us
    psum x1, blocking collectives, local_step(): weight_all = lax.psum(weight_sum * rescale, 'sp')  46 us
    dot_general x1, matrix products, local_step(): jnp.dot(tokens, w_query, preferred_element_type=jnp.float32)  13.6 us
  transfers between devices with their start and end apart: 1, of which 1 were waited for; matrix products, arithmetic and copies ran while one was open for 0% of the time, Pallas kernels for 0%

commit v1 on v0

v1 whole, which is shorter than its diff:
```python
import functools

import jax
import jax.numpy as jnp
from jax import lax
from jax.experimental import pallas as pl
from jax.experimental.pallas import tpu as pltpu
from jax.sharding import PartitionSpec as P

F32, BF16 = jnp.float32, jnp.bfloat16
MESH = pl.DeviceIdType.MESH
LOWEST = float(jnp.finfo(jnp.float32).min)
STACK = 4
CHUNKS = 2
SPARE = 8


def attend_kernel(cfg, x_hbm, wq_hbm, wk_hbm, wv_hbm, wo_hbm, k_hbm, v_hbm, pos_ref, y_hbm, kn_hbm, vn_hbm,
                  xv, wq, wkv, wo, kc, vc, q_all, kv_new, kv_f32, q_f32, o_own, o_par, ml_own, ml_par,
                  o_send, o_recv, ml_send, ml_recv, y_own, y_out, y_par, y_send, y_recv, y_all,
                  in_sem, wq_sem, out_sem, yout_sem, q_sem, kv_sem, par_sem, ring_sem, mring_sem, ypar_sem, yring_sem, ag_sem, agp_sem):
    n_sp, n_rows, n_heads, hd, seq_local = cfg
    nz = n_sp // 2
    half = n_heads // 2
    hops = nz // 2
    rows = n_rows // CHUNKS
    pitch = n_rows + SPARE
    lt = hd // 128
    yblk = y_all.shape[2]
    per_tile = STACK * n_heads
    scale = hd ** -0.5
    me = lax.axis_index('sp')
    z, core = me // 2, me % 2
    other = 1 - core
    partner = {'sp': z * 2 + other}
    nbr = ({'sp': lax.rem(z + 1, nz) * 2 + core}, {'sp': lax.rem(z + nz - 1, nz) * 2 + core})

    def local(src, dst, sem):
        return pltpu.make_async_copy(src, dst, sem)

    x_in = local(x_hbm, xv, in_sem.at[0])
    x_in.start()

    def wq_in(i):
        col = pl.multiple_of((2 * i + core) * hd, hd)
        return local(wq_hbm.at[:, pl.ds(col, hd)], wq.at[i], wq_sem.at[i])

    for i in range(half):
        wq_in(i).start()

    @pl.when(core == 0)
    def _():
        local(wk_hbm, wkv, in_sem.at[1]).start()

    @pl.when(core == 1)
    def _():
        local(wv_hbm, wkv, in_sem.at[1]).start()

    k_in = local(k_hbm, kc, in_sem.at[2])
    v_in = local(v_hbm, vc, in_sem.at[3])
    k_in.start()
    v_in.start()
    d_model = y_hbm.shape[1]
    dh = d_model // 2
    wo_in = [local(wo_hbm.at[:, pl.ds(p * dh, dh)], wo.at[p], in_sem.at[4 + p]) for p in range(2)]
    for c in wo_in:
        c.start()

    barrier = pltpu.get_barrier_semaphore()
    for dev in (partner, *nbr):
        pl.semaphore_signal(barrier, inc=1, device_id=dev, device_id_type=MESH)
    pl.semaphore_wait(barrier, 3)

    def remote(src, dst, sems, dev):
        return pltpu.make_async_remote_copy(src_ref=src, dst_ref=dst, send_sem=sems.at[0], recv_sem=sems.at[1],
                                            device_id=dev, device_id_type=MESH)

    def q_copy(i, c):
        g = c * half + i
        return remote(q_all.at[g], q_all.at[g], q_sem.at[i], partner)

    def widen(g, q):
        r = pl.ds(pl.multiple_of(g * pitch, 8), n_rows)
        for i in range(lt):
            q_f32[i, r, :] = q[:, i * 128:(i + 1) * 128].astype(F32)

    x_in.wait()

    def q_head(i, carry):
        wq_in(i).wait()
        q = jnp.dot(xv[...], wq[i], preferred_element_type=F32).astype(BF16)
        g = core * half + i
        q_all[g] = q
        q_copy(i, core).start()
        widen(g, q)
        return carry

    lax.fori_loop(0, half, q_head, 0)
    local(wk_hbm, wkv, in_sem.at[1]).wait()
    kv_new[core] = jnp.dot(xv[...], wkv[...], preferred_element_type=F32).astype(BF16)
    kv_copy = remote(kv_new.at[core], kv_new.at[core], kv_sem, partner)
    kv_copy.start()

    def q_other(i, carry):
        q_copy(i, core).wait()
        g = other * half + i
        widen(g, q_all[g])
        return carry

    lax.fori_loop(0, half, q_other, 0)
    kv_copy.wait()
    kv_f32[...] = kv_new[...].astype(F32)
    kv_out = [local(kv_new.at[0], kn_hbm, out_sem.at[0]), local(kv_new.at[1], vn_hbm, out_sem.at[1])]
    for c in kv_out:
        c.start()
    k_in.wait()
    v_in.wait()

    width = STACK * seq_local
    row_seq = lax.broadcasted_iota(jnp.int32, (per_tile, 1), 0) // n_heads
    col = lax.broadcasted_iota(jnp.int32, (1, width), 1)
    col_seq, col_t = col // seq_local, col % seq_local
    lane = lax.broadcasted_iota(jnp.int32, (per_tile, 128), 1)
    base = me * seq_local

    def tile(j, carry):
        b0 = j * STACK
        slots = [pos_ref[b0 + s] - base for s in range(STACK)]
        slot_col, slot_row = jnp.full((1, width), slots[0]), jnp.full((per_tile, 1), slots[0])
        for s in range(1, STACK):
            slot_col = jnp.where(col_seq == s, slots[s], slot_col)
            slot_row = jnp.where(row_seq == s, slots[s], slot_row)
        keep = (row_seq == col_seq) & (col_t < slot_col)
        holds = (slot_row >= 0) & (slot_row < seq_local)
        q = jnp.concatenate([jnp.concatenate([q_f32[i, pl.ds(b0 + s, n_heads, stride=pitch), :] for i in range(lt)], axis=1)
                             for s in range(STACK)], axis=0)
        kn = jnp.concatenate([jnp.broadcast_to(kv_f32[0, pl.ds(b0 + s, 1), :], (n_heads, hd)) for s in range(STACK)], axis=0)
        vn = jnp.concatenate([jnp.broadcast_to(kv_f32[1, pl.ds(b0 + s, 1), :], (n_heads, hd)) for s in range(STACK)], axis=0)
        sc = lax.dot_general(q.astype(BF16), kc[j], (((1,), (1,)), ((), ())), preferred_element_type=F32) * scale
        sc = jnp.where(keep, sc, -jnp.inf)
        s_new = jnp.sum(q * kn, axis=1, keepdims=True) * scale
        s_new = jnp.where(holds, s_new, -jnp.inf)
        peak = jnp.maximum(jnp.maximum(jnp.max(sc, axis=1, keepdims=True), s_new), LOWEST)
        w = jnp.exp(sc - peak)
        w_new = jnp.exp(s_new - peak)
        total = jnp.sum(w, axis=1, keepdims=True) + w_new
        o = jnp.dot(w.astype(BF16), vc[j], preferred_element_type=F32) + w_new.astype(BF16).astype(F32) * vn
        ml = jnp.where(lane == 0, peak, total)
        for s in range(STACK):
            at = pl.ds(b0 + s, n_heads, stride=pitch)
            for i in range(lt):
                o_own[i, at, :] = o[s * n_heads:(s + 1) * n_heads, i * 128:(i + 1) * 128]
            ml_own[at, :] = ml[s * n_heads:(s + 1) * n_heads]
        return carry

    def part_rows(i, ch):
        return pl.ds(pl.multiple_of(i * pitch + ch * rows, 8), rows)

    def par_copies(i, ch):
        src, dst = part_rows(other * half + i, ch), part_rows(i, ch)
        return (remote(o_own.at[:, src], o_par.at[:, dst], par_sem.at[0, i, ch], partner),
                remote(ml_own.at[src], ml_par.at[dst], par_sem.at[1, i, ch], partner))

    tiles = n_rows // STACK // CHUNKS
    for ch in range(CHUNKS):
        lax.fori_loop(ch * tiles, (ch + 1) * tiles, tile, 0)
        for i in range(half):
            for c in par_copies(i, ch):
                c.start()

    for ch in range(CHUNKS):
        for i in range(half):
            for c in par_copies(i, ch):
                c.wait()

    lane_r = lax.broadcasted_iota(jnp.int32, (rows, 128), 1)
    row_r = lax.broadcasted_iota(jnp.int32, (rows, 128), 0)

    def to_row(m, l):
        return jnp.sum(jnp.where(lane_r == row_r, m, jnp.where(lane_r == row_r + 64, l, 0.0)), axis=0, keepdims=True)

    def to_cols(ml):
        m = jnp.sum(jnp.where(lane_r == row_r, ml, 0.0), axis=1, keepdims=True)
        l = jnp.sum(jnp.where(lane_r == row_r + 64, ml, 0.0), axis=1, keepdims=True)
        return m, l

    def own_terms(d, ch):
        a, b = part_rows(core * half + d, ch), part_rows(d, ch)
        return [([o_own[i, a, :] for i in range(lt)], ml_own[a, 0:1], ml_own[a, 1:2]),
                ([o_par[i, b, :] for i in range(lt)], ml_par[b, 0:1], ml_par[b, 1:2])]

    def merge(terms):
        top = functools.reduce(jnp.maximum, [m for _, m, _ in terms])
        f = [jnp.exp(m - top) for _, m, _ in terms]
        o = [sum(t[0][i] * f_t for t, f_t in zip(terms[1:], f[1:])) + terms[0][0][i] * f[0] for i in range(lt)]
        return o, top, sum(t[2] * f_t for t, f_t in zip(terms, f))

    def ring_copies(w, t, ch):
        return (remote(o_send.at[w, t, ch], o_recv.at[w, t, ch], ring_sem.at[w, t, ch], nbr[w]),
                remote(ml_send.at[w, t, ch], ml_recv.at[w, t, ch], mring_sem.at[w, t, ch], nbr[w]))

    def sends(w, t, ch):
        return t > 0 or ch % 2 == w

    def dest(w, t):
        dist = hops - t
        return lax.rem(z + (dist if w == 0 else nz - dist), nz)

    def received(w, t, ch):
        for c in ring_copies(w, t, ch):
            c.wait_recv()
        m, l = to_cols(ml_recv[w, t, ch])
        return ([o_recv[w, t, ch, i] for i in range(lt)], m, l)

    for t in range(hops):
        for ch in range(CHUNKS):
            for w in range(2):
                if not sends(w, t, ch):
                    continue
                terms = own_terms(dest(w, t), ch)
                if t > 0 and sends(w, t - 1, ch):
                    terms.append(received(w, t - 1, ch))
                o, m, l = merge(terms)
                for i in range(lt):
                    o_send[w, t, ch, i] = o[i]
                ml_send[w, t, ch] = to_row(m, l)
                for c in ring_copies(w, t, ch):
                    c.start()

    for c in wo_in:
        c.wait()

    def ypar_copy(i, ch):
        return remote(y_out.at[i, pl.ds(ch * rows, rows)], y_par.at[i, pl.ds(ch * rows, rows)], ypar_sem.at[i, ch], partner)

    for ch in range(CHUNKS):
        o, _, l = merge(own_terms(z, ch) + [received(w, hops - 1, ch) for w in range(2)])
        head = jnp.concatenate([o_i / l for o_i in o], axis=1).astype(BF16)
        there = jnp.dot(head, wo[other], preferred_element_type=F32)
        for i in range(nz):
            y_out[i, pl.ds(ch * rows, rows), :] = there[:, i * yblk:(i + 1) * yblk]
        for i in range(nz):
            ypar_copy(i, ch).start()
        here = jnp.dot(head, wo[core], preferred_element_type=F32)
        for i in range(nz):
            y_own[i, pl.ds(ch * rows, rows), :] = here[:, i * yblk:(i + 1) * yblk]

    def yring_copy(w, t, ch):
        return remote(y_send.at[w, t, ch], y_recv.at[w, t, ch], yring_sem.at[w, t, ch], nbr[w])

    for ch in range(CHUNKS):
        for i in range(nz):
            ypar_copy(i, ch).wait()

    def y_terms(d, ch):
        r = pl.ds(ch * rows, rows)
        return y_own[d, r, :] + y_par[d, r, :]

    for t in range(hops):
        for ch in range(CHUNKS):
            for w in range(2):
                if not sends(w, t, ch):
                    continue
                part = y_terms(dest(w, t), ch)
                if t > 0 and sends(w, t - 1, ch):
                    yring_copy(w, t - 1, ch).wait_recv()
                    part = part + y_recv[w, t - 1, ch]
                y_send[w, t, ch] = part
                yring_copy(w, t, ch).start()

    def ag_copy(w, t, ch):
        src = lax.rem(z + (nz - t if w == 0 else t), nz)
        ref = y_all.at[core * half + src, pl.ds(ch * rows, rows)]
        return remote(ref, ref, ag_sem.at[w, t, ch], nbr[w])

    def ag_recv(w, t, ch):
        src = lax.rem(z + (nz - t - 1 if w == 0 else t + 1), nz)
        ref = y_all.at[core * half + src, pl.ds(ch * rows, rows)]
        return remote(ref, ref, ag_sem.at[w, t, ch], nbr[w])

    def agp_copy(src, ch, c):
        ref = y_all.at[c * half + src, pl.ds(ch * rows, rows)]
        return remote(ref, ref, agp_sem.at[src, ch], partner)

    def y_block_out(c, src, ch):
        r = pl.ds(ch * rows, rows)
        at = pl.multiple_of((c * half + src) * yblk, yblk)
        return local(y_all.at[c * half + src, r], y_hbm.at[r, pl.ds(at, yblk)], yout_sem.at[c, src, ch])

    def gathers(w, t, ch):
        return t < hops - 1 or ch % 2 == w

    for ch in range(CHUNKS):
        part = y_terms(z, ch)
        for w in range(2):
            yring_copy(w, hops - 1, ch).wait_recv()
            part = part + y_recv[w, hops - 1, ch]
        y_all[core * half + z, pl.ds(ch * rows, rows), :] = part.astype(BF16)
        for w in range(2):
            if gathers(w, 0, ch):
                ag_copy(w, 0, ch).start()
        agp_copy(z, ch, core).start()
        y_block_out(core, z, ch).start()

    for t in range(hops):
        for ch in range(CHUNKS):
            for w in range(2):
                if not gathers(w, t, ch):
                    continue
                ag_recv(w, t, ch).wait_recv()
                if t + 1 < hops and gathers(w, t + 1, ch):
                    ag_copy(w, t + 1, ch).start()
                src = lax.rem(z + (nz - t - 1 if w == 0 else t + 1), nz)
                agp_copy(src, ch, core).start()
                y_block_out(core, src, ch).start()

    def order():
        yield z
        for t in range(hops):
            yield lax.rem(z + nz - t - 1, nz)
            if t < hops - 1:
                yield lax.rem(z + t + 1, nz)

    for src in order():
        for ch in range(CHUNKS):
            agp_copy(src, ch, other).wait_recv()
            y_block_out(other, src, ch).start()

    for src in range(nz):
        for ch in range(CHUNKS):
            agp_copy(src, ch, core).wait_send()
            for c in range(2):
                y_block_out(c, src, ch).wait()
    for t in range(hops):
        for ch in range(CHUNKS):
            for w in range(2):
                if sends(w, t, ch):
                    for c in ring_copies(w, t, ch):
                        c.wait_send()
                    yring_copy(w, t, ch).wait_send()
                if gathers(w, t, ch):
                    ag_copy(w, t, ch).wait_send()
    for c in kv_out:
        c.wait()


def attend(cfg, *args):
    n_sp, n_rows, n_heads, hd, seq_local = cfg
    x, w_query, w_key, w_value, w_out, k, v, pos = args
    nz, half, hops, rows = n_sp // 2, n_heads // 2, n_sp // 4, n_rows // CHUNKS
    d_model, yblk, stacks = x.shape[1], w_out.shape[1] // n_sp, n_rows // STACK
    width, pitch, lt = STACK * seq_local, n_rows + SPARE, hd // 128
    dma = lambda *s: pltpu.SemaphoreType.DMA(s)
    any_spec = pl.BlockSpec(memory_space=pl.ANY)
    return pl.pallas_call(
        functools.partial(attend_kernel, cfg),
        name='attend',
        out_shape=(jax.ShapeDtypeStruct((n_rows, w_out.shape[1]), BF16),
                   jax.ShapeDtypeStruct((n_rows, hd), BF16),
                   jax.ShapeDtypeStruct((n_rows, hd), BF16)),
        in_specs=[any_spec] * 7 + [pl.BlockSpec(memory_space=pltpu.SMEM)],
        out_specs=(any_spec,) * 3,
        scratch_shapes=[
            pltpu.VMEM((n_rows, d_model), BF16),
            pltpu.VMEM((half, d_model, hd), BF16),
            pltpu.VMEM((d_model, hd), BF16),
            pltpu.VMEM((2, hd, w_out.shape[1] // 2), BF16),
            pltpu.VMEM((stacks, width, hd), BF16),
            pltpu.VMEM((stacks, width, hd), BF16),
            pltpu.VMEM((n_heads, n_rows, hd), BF16),
            pltpu.VMEM((2, n_rows, hd), BF16),
            pltpu.VMEM((2, n_rows, hd), F32),
            pltpu.VMEM((lt, n_heads * pitch, 128), F32),
            pltpu.VMEM((lt, n_heads * pitch, 128), F32),
            pltpu.VMEM((lt, half * pitch, 128), F32),
            pltpu.VMEM((n_heads * pitch, 128), F32),
            pltpu.VMEM((half * pitch, 128), F32),
            pltpu.VMEM((2, hops, CHUNKS, lt, rows, 128), F32),
            pltpu.VMEM((2, hops, CHUNKS, lt, rows, 128), F32),
            pltpu.VMEM((2, hops, CHUNKS, 1, 128), F32),
            pltpu.VMEM((2, hops, CHUNKS, 1, 128), F32),
            pltpu.VMEM((nz, n_rows, yblk), F32),
            pltpu.VMEM((nz, n_rows, yblk), F32),
            pltpu.VMEM((nz, n_rows, yblk), F32),
            pltpu.VMEM((2, hops, CHUNKS, rows, yblk), F32),
            pltpu.VMEM((2, hops, CHUNKS, rows, yblk), F32),
            pltpu.VMEM((n_sp, n_rows, yblk), BF16),
            dma(6), dma(half), dma(2), dma(2, nz, CHUNKS),
            dma(half, 2), dma(2), dma(2, half, CHUNKS, 2),
            dma(2, hops, CHUNKS, 2), dma(2, hops, CHUNKS, 2), dma(nz, CHUNKS, 2),
            dma(2, hops, CHUNKS, 2), dma(2, hops, CHUNKS, 2), dma(nz, CHUNKS, 2),
        ],
        compiler_params=pltpu.CompilerParams(collective_id=0, has_side_effects=True, vmem_limit_bytes=60 * 1024 * 1024),
        cost_estimate=pl.CostEstimate(flops=10**9, bytes_accessed=3 * 10**7, transcendentals=0),
    )(x, w_query, w_key, w_value, w_out, k.reshape(stacks, width, hd), v.reshape(stacks, width, hd), pos)


def solution(mesh):
    n_sp = mesh.shape['sp']

    def local_step(tokens, w_query, w_key, w_value, w_out, k_cache, v_cache, positions):
        n_rows, seq_local, hd = k_cache.shape
        cfg = (n_sp, n_rows, w_query.shape[1] // hd, hd, seq_local)
        attn_out, key_new, value_new = attend(cfg, tokens, w_query, w_key, w_value, w_out, k_cache, v_cache, positions)
        local_pos = positions - lax.axis_index('sp') * seq_local
        hit = (jnp.arange(seq_local)[None, :] == local_pos[:, None])[:, :, None]
        return attn_out, jnp.where(hit, key_new[:, None, :], k_cache), jnp.where(hit, value_new[:, None, :], v_cache)

    cache_spec = P('dp', 'sp', None)
    return jax.shard_map(local_step, mesh=mesh,
                         in_specs=(P('dp', None), P(), P(), P(), P('sp', None), cache_spec, cache_spec, P('dp')),
                         out_specs=(P('dp', None), cache_spec, cache_spec), check_vma=False)
```

time: 262 us -> 87.4 us (0.33)
  the two profiles are of different devices: /device:TPU:22 before, /device:TPU:21 now
where the time goes in v1:
time: 87.4 us; the launch traced here: 87.2 us
  Pallas kernels  79.5 us (91%)
  other arithmetic  6.15 us (7%)
  local copies, waits for them, and re-layouts  0.89 us (1%)
    pallas_call x1, Pallas kernels, attend(): pl.pallas_call(functools.partial(attend_kernel, cfg), name='attend', out_...  79.5 us
    select_n x1, other arithmetic, local_step(): jnp.where(hit, value_new[:, None, :], v_cache)  5.41 us

profile of v1, /device:TPU:21, one launch (start us, length us, event | category | flops | bytes accessed | tf_op | source)
XLA Modules:
  0.0 87.2 jit_solution(1915152029400032972)
XLA Ops:
  0.6 0.7 broadcast_subtract_fusion
  1.3 0.1 iota_compare_fusion
  1.4 0.0 copy-start
  1.4 79.5 %attend.1 = (bf16[96,4096]{1,0:T(8,128)(2,1)}, bf16[96,256]{1,0:T(8,128)(2,1)}, bf16[96,256]{1,0:T(8,128)(2,1)}) custom-call(bf16[96,4096]{1,0:T(8,128)(2,1)} %x_hbm.1, bf16[4096,4096]{1,0:T(8,128)(2,1)} %wq_hbm.1, bf16[4096,256]{1,0:T(8,128)(2,1)} %wk_hbm.1, bf16[4096,256]{1,0:T(8,128)(2,1)} %wv_hbm.1, bf16[256,4096]{1,0:T(8,128)(2,1)} %wo_hbm.1, ...), custom_call_target="tpu_custom_call" | custom-call | flops 1000000000 | bytes 30000000 | tf_op jit(solution)/shard_map/attend/pallas_call | solution.py:355
  80.9 0.0 copy-done
  80.9 0.0 copy-start.1
  80.9 5.4 %broadcast_select_fusion = (bf16[96,64,256]{2,1,0:T(8,128)(2,1)}, bf16[96,64,256]{2,1,0:T(8,128)(2,1)}) fusion(bf16[96,64,256]{2,1,0:T(8,128)(2,1)} %param.14, pred[96,64]{1,0:T(8,128)(4,1)S(1)} %iota_compare_fusion, bf16[96,256]{1,0:T(8,128)(2,1)} %get-tuple-element.8, bf16[96,64,256]{2,1,0:T(8,128)(2,1)S(1)} %copy-done, bf16[96,256]{1,0:T(8,128)(2,1)} %get-tuple-element.7), kind=kLoop, calls=%fused_computation | loop fusion | flops 3145728 | bytes 12687360 | tf_op jit(solution)/shard_map/jit(_where)/select_n | solution.py:407
  86.3 0.0 copy-done.1
  86.3 0.9 %copy.12 = bf16[96,4096]{1,0:T(8,128)(2,1)} copy(bf16[96,4096]{1,0:T(8,128)(2,1)S(1)} %copy-done.1) | data formatting | bytes 1572864
Async XLA Ops:
  1.4 79.5 %copy-start = (bf16[96,64,256]{2,1,0:T(8,128)(2,1)S(1)}, bf16[96,64,256]{2,1,0:T(8,128)(2,1)}, u32[]{:S(2)}) copy-start(bf16[96,64,256]{2,1,0:T(8,128)(2,1)} %param.13) | copy-start | bytes 9437188
  80.9 5.4 %copy-start.1 = (bf16[96,4096]{1,0:T(8,128)(2,1)S(1)}, bf16[96,4096]{1,0:T(8,128)(2,1)}, u32[]{:S(2)}) copy-start(bf16[96,4096]{1,0:T(8,128)(2,1)} %get-tuple-element.14) | copy-start | bytes 2359300
